TPU v7x, 32 devices: a whole 2x2x4 slice. The times are simulated.
32 devices in a mesh: grp: 4 (over z), dev: 8 (over y, x, core).
Axes of the slice: x: 2, y: 2, z: 4, core: 2. Of those that a mesh axis runs over, the one named last changes fastest.
Arguments:
- matrix_tiles: bfloat16 [640, 128, 1024], P(('grp', 'dev')), may hold values from -0.125 to 0.125
- tile_column: int32 [640], P(('grp', 'dev')), may hold values from 0 to 255
- block_counts: int32 [256], P(('grp', 'dev')), may hold values from 1 to 4, as said below
- destination: int32 [256], P(('grp', 'dev')), may hold values from 0 to 7, as said below
- row_bounds: bfloat16 [32768], P(('grp', 'dev')), may hold values from -6 to 6
- dual_start: bfloat16 [32768], P(('grp', 'dev')), may hold values from 0 to 1
- primal_start: float32 [262144], replicated, may hold values from 0 to 0.5
- cost_vector: float32 [262144], replicated, may hold values from -6 to 6
- upper_bound: float32 [262144], replicated, may hold values from 0.5 to 2
Outputs:
- primal_final: float32 [262144], replicated
- dual_final: float32 [32768], P(('grp', 'dev'))
- weight_final: float32 [1], replicated
Inputs may be any that keep to these rules, and one draw needn't show every extreme that they name: `block_counts`: each device's 8 row blocks have 1 to 4 tiles each and 20 at most together; some device has exactly 20 in every draw. `destination`: on every device the 8 entries are each of 0 to 7 once.
All inputs are finite; a program needn't handle non-finite values.
Results may differ from a plain program's by a relative error of at most 0.0015.
Values may be sent and summed in bfloat16 or wider, within the bound.
A program may use at most 128 MiB of HBM per device.

v0:
```python
import jax
import jax.numpy as jnp
from jax import lax
from jax.sharding import PartitionSpec as P

NCB = 256
ITERS = 3
step_scale = 0.3


def row_products(tile_store, vector_bf, blocks):
    tile_set, tile_cols, owners, live_flags = tile_store
    vector_table = vector_bf.reshape(-1, tile_set.shape[2])
    column_hot = (
        tile_cols[:, None] == jnp.arange(vector_table.shape[0], dtype=jnp.int32)[None, :]
    ).astype(jnp.bfloat16)
    picked = jnp.dot(column_hot, vector_table, preferred_element_type=jnp.float32).astype(
        jnp.bfloat16
    )
    product = jnp.einsum("src,sc->sr", tile_set, picked, preferred_element_type=jnp.float32)
    product = jnp.where(live_flags[:, None], product, 0.0)
    owner_hot = (jnp.arange(blocks, dtype=jnp.int32)[:, None] == owners[None, :]).astype(
        jnp.float32
    )
    return jnp.dot(owner_hot, product, precision=lax.Precision.HIGHEST)


def column_products(tile_store, rows_bf):
    tile_set, tile_cols, owners, live_flags = tile_store
    blocks = rows_bf.shape[0]
    owner_hot = (owners[:, None] == jnp.arange(blocks, dtype=jnp.int32)[None, :]).astype(
        jnp.bfloat16
    )
    picked_rows = jnp.dot(owner_hot, rows_bf, preferred_element_type=jnp.float32).astype(
        jnp.bfloat16
    )
    product = jnp.einsum("src,sr->sc", tile_set, picked_rows, preferred_element_type=jnp.float32)
    product = jnp.where(live_flags[:, None], product, 0.0)
    column_hot = (jnp.arange(NCB, dtype=jnp.int32)[:, None] == tile_cols[None, :]).astype(
        jnp.float32
    )
    return jnp.dot(column_hot, product, precision=lax.Precision.HIGHEST).reshape(-1)


def per_device(
    matrix_tiles,
    tile_column,
    block_counts,
    destination,
    row_bounds,
    dual_start,
    primal_start,
    cost_vector,
    upper_bound,
):
    blocks = block_counts.shape[0]
    rows_per = matrix_tiles.shape[1]
    slot_count = matrix_tiles.shape[0]
    starts = jnp.cumsum(block_counts) - block_counts
    slot_ids = jnp.arange(slot_count, dtype=jnp.int32)
    owners = jnp.sum((starts[None, 1:] <= slot_ids[:, None]).astype(jnp.int32), axis=1)
    bounds_here = row_bounds.reshape(blocks, rows_per)
    dual_here = dual_start.reshape(blocks, rows_per)
    peer_ids = jnp.arange(blocks, dtype=jnp.int32)
    inverse = jnp.sum(
        jnp.where(destination[None, :] == peer_ids[:, None], peer_ids[None, :], 0), axis=1
    )
    tile_store = (matrix_tiles, tile_column, owners, slot_ids < jnp.sum(block_counts))
    bounds = bounds_here.astype(jnp.float32)
    dual_state = dual_here.astype(jnp.float32)
    primal = primal_start
    weight = jnp.ones((), jnp.float32)
    row_image = row_products(tile_store, primal.astype(jnp.bfloat16), blocks)
    for iteration in range(ITERS):
        step_primal = step_scale / weight
        step_dual = step_scale * weight
        partial_value = column_products(tile_store, dual_state.astype(jnp.bfloat16))
        gradient = lax.psum(partial_value, ("grp", "dev"))
        primal_next = jnp.clip(primal - step_primal * (cost_vector - gradient), 0.0, upper_bound)
        change = jnp.sum((primal_next - primal) ** 2)
        next_image = row_products(tile_store, primal_next.astype(jnp.bfloat16), blocks)
        dual_state = jnp.maximum(
            dual_state + step_dual * (bounds - (2.0 * next_image - row_image)), 0.0
        )
        violation_part = jnp.sum(jnp.maximum(bounds - next_image, 0.0) ** 2)
        violation = lax.psum(violation_part, ("grp", "dev"))
        weight = jnp.sqrt(weight * jnp.sqrt((violation + 1e-06) / (change + 1e-06)))
        primal = primal_next
        row_image = next_image
    dual_final = lax.all_to_all(
        dual_state[inverse], "dev", split_axis=0, concat_axis=0, tiled=True
    ).reshape(-1)
    return (primal, dual_final, jnp.reshape(weight, (1,)))


def solution(mesh):
    in_specs = (
        P(("grp", "dev"), None, None),
        P(("grp", "dev")),
        P(("grp", "dev")),
        P(("grp", "dev")),
        P(("grp", "dev")),
        P(("grp", "dev")),
        P(),
        P(),
        P(),
    )
    out_specs = (P(), P(("grp", "dev")), P())
    return jax.shard_map(
        per_device, mesh=mesh, in_specs=in_specs, out_specs=out_specs, check_vma=False
    )
```

profile of v0, /device:TPU:0, one launch (start us, length us, event | category | flops | bytes accessed | tf_op | source)
XLA Modules:
  0.0 506.8 jit_solution(13658657499883403431)
XLA Ops:
  7.2 0.0 copy-start.5
  7.2 0.0 copy-start.1
  7.2 0.0 all-reduce.4.cloned.1.call-start
  7.2 1.0 reduce-window.9
  8.2 1.3 fusion.92
  9.5 0.1 slice.3
  9.6 0.1 convert_reduce_fusion
  9.7 0.6 iota_compare_fusion.20
  10.3 0.9 fusion.4
  11.2 3.3 fusion.46
  14.5 0.6 convolution_bitcast_fusion.2
  15.1 1.2 copy.28
  16.3 0.0 all-reduce.4.cloned.1.call-update
  16.3 0.0 all-reduce.6.cloned.1.call-start
  16.3 133.6 %all-reduce.4.cloned.1.call-done = f32[262144]{0:T(1024)} async-done(((f32[262144]{0:T(1024)}), f32[262144]{0:T(1024)}) %all-reduce.4.cloned.1.call-update) | async-done | bytes 1048592 | tf_op jit(solution)/shard_map/psum | solution.py:78
  149.9 3.5 multiply_reduce_fusion.2
  153.5 0.1 convert_element_type.70
  153.5 1.0 reshape.95
  154.6 1.3 fusion
  155.8 0.0 copy-start.6
  155.8 4.0 fusion.20
  159.8 0.2 reshape.96
  160.0 0.2 fusion.1
  160.2 3.9 fusion.18
  164.2 0.0 copy-done.7
  164.2 0.8 fusion.61
  165.0 0.0 copy-done.6
  165.0 0.2 fusion.10
  165.2 0.2 fusion.5
  165.4 3.3 fusion.44
  168.7 0.6 convolution_bitcast_fusion.1
  169.3 1.2 copy.29
  170.5 0.0 all-reduce.6.cloned.1.call-update
  170.5 0.0 all-reduce.8.cloned.1.call-start
  170.6 39.6 %psum.43 = f32[]{:T(128)} all-reduce(f32[]{:T(128)} %get-tuple-element.14), channel_id=1, replica_groups=mesh['grp'=4,'dev'=8] {'grp','dev'}, use_global_device_ids=true, to_apply=%region_5.6 | all-reduce | flops 1 | bytes 8 | tf_op jit(solution)/shard_map/psum | solution.py:86
  211.7 88.9 %all-reduce.6.cloned.1.call-done = f32[262144]{0:T(1024)} async-done(((f32[262144]{0:T(1024)}), f32[262144]{0:T(1024)}) %all-reduce.6.cloned.1.call-update) | async-done | bytes 1048592 | tf_op jit(solution)/shard_map/psum | solution.py:78
  300.6 2.4 multiply_reduce_fusion.1
  303.0 0.1 convert_element_type.77
  303.0 0.2 reshape.98
  303.3 0.2 fusion.2
  303.5 3.9 fusion.16
  307.4 0.8 fusion.64
  308.3 0.2 fusion.6
  308.4 3.3 fusion.42
  311.7 0.6 convolution_bitcast_fusion
  312.4 1.2 copy.30
  313.5 0.0 all-reduce.8.cloned.1.call-update
  313.5 0.0 copy-done.8
  313.5 0.1 select_reduce_fusion
  313.7 39.9 %psum.45 = f32[]{:T(128)} all-reduce(f32[]{:T(128)} %get-tuple-element.16), channel_id=1, replica_groups=mesh['grp'=4,'dev'=8] {'grp','dev'}, use_global_device_ids=true, to_apply=%region_9.10 | all-reduce | flops 1 | bytes 8 | tf_op jit(solution)/shard_map/psum | solution.py:86
  355.0 88.6 %all-reduce.8.cloned.1.call-done = f32[262144]{0:T(1024)} async-done(((f32[262144]{0:T(1024)}), f32[262144]{0:T(1024)}) %all-reduce.8.cloned.1.call-update) | async-done | bytes 1048592 | tf_op jit(solution)/shard_map/psum | solution.py:78
  443.6 0.0 copy-done.2
  443.6 2.1 multiply_reduce_fusion
  445.7 1.0 copy-done.3
  446.7 0.1 convert_element_type.81
  446.7 0.2 reshape.100
  446.9 0.2 fusion.3
  447.2 3.9 fusion.14
  451.1 0.9 fusion.73
  452.0 1.1 gather_fusion
  453.2 3.6 all-to-all-start
  456.7 40.5 %psum.47 = f32[]{:T(128)} all-reduce(f32[]{:T(128)} %get-tuple-element.10), channel_id=1, replica_groups=mesh['grp'=4,'dev'=8] {'grp','dev'}, use_global_device_ids=true, to_apply=%region_14.15 | all-reduce | flops 1 | bytes 8 | tf_op jit(solution)/shard_map/psum | solution.py:86
  498.5 0.0 all-to-all-done
  498.6 0.6 copy.83
  (12 shorter events, 0.0 us)
Async XLA Ops:
  7.2 7.3 %copy-start.5 = (s32[20]{0:T(128)S(1)}, s32[20]{0:T(128)}, u32[]{:S(2)}) copy-start(s32[20]{0:T(128)} %param.10) | copy-start | bytes 244
  7.2 142.8 %copy-start.1 = (f32[262144]{0:T(1024)S(1)}, f32[262144]{0:T(1024)}, u32[]{:S(2)}) copy-start(f32[262144]{0:T(1024)} %param.16) | copy-start | bytes 3145732
  7.2 142.8 %copy-start = (f32[262144]{0:T(1024)S(1)}, f32[262144]{0:T(1024)}, u32[]{:S(2)}) copy-start(f32[262144]{0:T(1024)} %param.17) | copy-start | bytes 3145732
  7.2 142.7 %all-reduce.4.cloned.1.call-start = ((), (), s32[]{:S(2)}) async-start(), calls=%async_computation.1 | async-start | bytes 2097152 | tf_op jit(solution)/shard_map/psum | solution.py:78
  16.3 284.3 %all-reduce.6.cloned.1.call-start = ((), (), s32[]{:S(2)}) async-start(), calls=%async_computation.2 | async-start | bytes 2097152 | tf_op jit(solution)/shard_map/psum | solution.py:78
  153.5 6.3 %copy-start.4 = (bf16[262144]{0:T(1024)(128)(2,1)S(1)}, bf16[262144]{0:T(1024)(128)(2,1)}, u32[]{:S(2)}) copy-start(bf16[262144]{0:T(1024)(128)(2,1)} %get-tuple-element.9) | copy-start | bytes 1572868
  155.8 8.4 %copy-start.7 = (bf16[1024]{0:T(1024)(128)(2,1)S(1)}, bf16[1024]{0:T(1024)(128)(2,1)}, u32[]{:S(2)}) copy-start(bf16[1024]{0:T(1024)(128)(2,1)} %param.13) | copy-start | bytes 6148
  155.8 9.2 %copy-start.6 = (bf16[1024]{0:T(1024)(128)(2,1)S(1)}, bf16[1024]{0:T(1024)(128)(2,1)}, u32[]{:S(2)}) copy-start(bf16[1024]{0:T(1024)(128)(2,1)} %param.14) | copy-start | bytes 6148
  170.5 273.1 %all-reduce.8.cloned.1.call-start = ((), (), s32[]{:S(2)}) async-start(), calls=%async_computation.3 | async-start | bytes 2097152 | tf_op jit(solution)/shard_map/psum | solution.py:78
  307.4 6.1 %copy-start.8 = (s32[8]{0:T(128)S(1)}, s32[8]{0:T(128)}, u32[]{:S(2)}) copy-start(s32[8]{0:T(128)} %param.12) | copy-start | bytes 100
  307.4 136.2 %copy-start.2 = (f32[262144]{0:T(1024)S(1)}, f32[262144]{0:T(1024)}, u32[]{:S(2)}) copy-start(f32[262144]{0:T(1024)} %param.16) | copy-start | bytes 3145732
  445.7 1.0 copy-start.3
  453.2 45.4 %all-to-all-start = ((f32[8,1,128]{2,1,0:T(1,128)}), f32[8,1,128]{2,1,0:T(1,128)S(1)}, u32[]{:S(2)}, u32[]{:S(2)}) async-start(f32[8,1,128]{2,1,0:T(1,128)} %bitcast.22), calls=%async_computation | async-start | bytes 8192 | tf_op jit(solution)/shard_map/all_to_all | solution.py:90
Sparse Core Ops, SparseCore 0:
  16.4 133.4 all-reduce.3
  170.6 129.8 all-reduce.5
  313.7 129.8 all-reduce.7
where the time goes:
time: 508 us; the launch traced here: 507 us
  waiting for transfers between devices  311 us (61%)
  blocking collectives  120 us (24%)
  matrix products  33.4 us (7%)
  between operations  19.3 us (4%)
  other arithmetic  11.3 us (2%)
  local copies, waits for them, and re-layouts  8.01 us (2%)
    psum x3, waiting for transfers between devices, per_device(): gradient = lax.psum(partial_value, ('grp', 'dev'))  311 us
    psum x3, blocking collectives, per_device(): violation = lax.psum(violation_part, ('grp', 'dev'))  120 us
    dot_general x4, matrix products, row_products(): jnp.einsum('src,sc->sr', tile_set, picked, preferred_element_type=jnp.flo...  15.8 us
  transfers between devices with their start and end apart: 4, of which 3 were waited for; matrix products, arithmetic and copies ran while one was open for 0% of the time, Pallas kernels for 0%

commit v1 on v0

--- a/solution.py
+++ b/solution.py
@@ -75,7 +75,8 @@
         step_primal = step_scale / weight
         step_dual = step_scale * weight
         partial_value = column_products(tile_store, dual_state.astype(jnp.bfloat16))
-        gradient = lax.psum(partial_value, ("grp", "dev"))
+        parts = lax.all_gather(partial_value, ("grp", "dev"))
+        gradient = jnp.sum(parts, axis=0)
         primal_next = jnp.clip(primal - step_primal * (cost_vector - gradient), 0.0, upper_bound)
         change = jnp.sum((primal_next - primal) ** 2)
         next_image = row_products(tile_store, primal_next.astype(jnp.bfloat16), blocks)

time: 508 us -> 771 us (1.52)
  waiting for transfers between devices: 311 us -> 498 us
  other arithmetic: 11.3 us -> 81.1 us
    all_gather x0 -> x3, waiting for transfers between devices: none -> 498 us  [per_device(): parts = lax.all_gather(partial_value, ('grp', 'dev'))]
    psum x3 -> x0, waiting for transfers between devices: 311 us -> none  [per_device(): gradient = lax.psum(partial_value, ('grp', 'dev'))]
    reduce_sum x0 -> x3, other arithmetic: none -> 69.8 us  [per_device(): gradient = jnp.sum(parts, axis=0)]
where the time goes in v1:
time: 771 us; the launch traced here: 770 us
  waiting for transfers between devices  498 us (65%)
  blocking collectives  123 us (16%)
  other arithmetic  81.1 us (11%)
  matrix products  33.4 us (4%)
  between operations  19.3 us (3%)
  local copies, waits for them, and re-layouts  11.2 us (1%)
    all_gather x3, waiting for transfers between devices, per_device(): parts = lax.all_gather(partial_value, ('grp', 'dev'))  498 us
    psum x3, blocking collectives, per_device(): violation = lax.psum(violation_part, ('grp', 'dev'))  123 us
    reduce_sum x3, other arithmetic, per_device(): gradient = jnp.sum(parts, axis=0)  69.8 us
    dot_general x4, matrix products, row_products(): jnp.einsum('src,sc->sr', tile_set, picked, preferred_element_type=jnp.flo...  15.8 us
  transfers between devices with their start and end apart: 4, of which 3 were waited for; matrix products, arithmetic and copies ran while one was open for 0% of the time, Pallas kernels for 0%

profile of v1, /device:TPU:0, one launch (start us, length us, event | category | flops | bytes accessed | tf_op | source)
XLA Modules:
  0.0 769.7 jit_solution(8297906791132501262)
XLA Ops:
  7.2 0.0 all-gather.7.cloned.1.call-start
  7.2 0.8 reduce-window.9
  8.1 1.3 fusion.95
  9.3 0.1 slice.3
  9.4 0.1 convert_reduce_fusion
  9.5 0.6 iota_compare_fusion.20
  10.2 0.9 fusion.4
  11.0 3.3 fusion.49
  14.3 0.6 fusion.13
  15.0 2.2 reshape.100
  17.2 0.0 all-gather.7.cloned.1.call-update
  17.2 0.0 copy-start
  17.2 0.0 copy-start.1
  17.2 0.0 all-gather.9.cloned.1.call-start
  17.3 197.0 %all-gather.7.cloned.1.call-done = f32[32,1,262144]{2,1,0:T(1,128)} async-done(((f32[1,1,262144]{2,1,0:T(1,128)}), f32[32,1,262144]{2,1,0:T(1,128)}) %all-gather.7.cloned.1.call-update) | async-done | bytes 33554448 | tf_op jit(solution)/shard_map/all_gather | solution.py:78
  214.2 23.3 %reduce_sum.112 = f32[262144]{0:T(1024)} reduce(f32[32,1,262144]{2,1,0:T(1,128)} %all-gather.7.cloned.1.call-done, f32[]{:T(128)} %constant.6.clone.1), dimensions={0,1}, to_apply=%region_3.4 | reduce | flops 8126464 | bytes 34603012 | tf_op jit(solution)/shard_map/reduce_sum | solution.py:79
  237.5 3.6 multiply_reduce_fusion.2
  241.1 0.1 convert_element_type.70
  241.2 1.0 reshape.85
  242.2 1.3 fusion
  243.4 0.0 copy-start.6
  243.5 4.0 fusion.23
  247.4 0.2 reshape.86
  247.7 0.2 fusion.1
  247.9 3.9 fusion.21
  251.8 0.8 fusion.64
  252.7 0.2 fusion.10
  252.8 0.2 fusion.5
  253.0 3.3 fusion.47
  256.3 0.6 fusion.12
  257.0 2.2 reshape.102
  259.2 0.0 all-gather.9.cloned.1.call-update
  259.2 0.0 all-gather.11.cloned.1.call-start
  259.3 41.6 %psum.21 = f32[]{:T(128)} all-reduce(f32[]{:T(128)} %get-tuple-element.14), channel_id=1, replica_groups=mesh['grp'=4,'dev'=8] {'grp','dev'}, use_global_device_ids=true, to_apply=%region_5.6 | all-reduce | flops 1 | bytes 8 | tf_op jit(solution)/shard_map/psum | solution.py:87
  302.4 150.6 %all-gather.9.cloned.1.call-done = f32[32,1,262144]{2,1,0:T(1,128)} async-done(((f32[1,1,262144]{2,1,0:T(1,128)}), f32[32,1,262144]{2,1,0:T(1,128)}) %all-gather.9.cloned.1.call-update) | async-done | bytes 33554448 | tf_op jit(solution)/shard_map/all_gather | solution.py:78
  453.0 23.3 %reduce_sum.115 = f32[262144]{0:T(1024)} reduce(f32[32,1,262144]{2,1,0:T(1,128)} %all-gather.9.cloned.1.call-done, f32[]{:T(128)} %constant.6.clone.1), dimensions={0,1}, to_apply=%region_7.8 | reduce | flops 8126464 | bytes 34603012 | tf_op jit(solution)/shard_map/reduce_sum | solution.py:79
  476.2 2.4 multiply_reduce_fusion.1
  478.6 0.1 convert_element_type.77
  478.7 0.2 reshape.87
  478.9 0.2 fusion.2
  479.1 3.9 fusion.19
  483.1 0.8 fusion.67
  483.9 0.2 fusion.6
  484.1 3.3 fusion.45
  487.4 0.6 fusion.11
  488.0 2.2 reshape.104
  490.2 0.0 all-gather.11.cloned.1.call-update
  490.3 0.1 select_reduce_fusion
  490.4 41.3 %psum.22 = f32[]{:T(128)} all-reduce(f32[]{:T(128)} %get-tuple-element.16), channel_id=1, replica_groups=mesh['grp'=4,'dev'=8] {'grp','dev'}, use_global_device_ids=true, to_apply=%region_9.10 | all-reduce | flops 1 | bytes 8 | tf_op jit(solution)/shard_map/psum | solution.py:87
  533.2 0.0 copy-start.2
  533.2 150.8 %all-gather.11.cloned.1.call-done = f32[32,1,262144]{2,1,0:T(1,128)} async-done(((f32[1,1,262144]{2,1,0:T(1,128)}), f32[32,1,262144]{2,1,0:T(1,128)}) %all-gather.11.cloned.1.call-update) | async-done | bytes 33554448 | tf_op jit(solution)/shard_map/all_gather | solution.py:78
  684.0 23.3 %reduce_sum.118 = f32[262144]{0:T(1024)} reduce(f32[32,1,262144]{2,1,0:T(1,128)} %all-gather.11.cloned.1.call-done, f32[]{:T(128)} %constant.6.clone.1), dimensions={0,1}, to_apply=%region_11.12 | reduce | flops 8126464 | bytes 34603012 | tf_op jit(solution)/shard_map/reduce_sum | solution.py:79
  707.2 2.1 multiply_reduce_fusion
  709.3 1.0 copy-done.3
  710.3 0.1 convert_element_type.81
  710.4 0.2 reshape.88
  710.6 0.2 fusion.3
  710.8 3.9 fusion.17
  714.8 0.9 fusion.76
  715.7 1.1 gather_fusion
  716.8 3.3 all-to-all-start
  720.1 40.0 %psum.23 = f32[]{:T(128)} all-reduce(f32[]{:T(128)} %get-tuple-element.10), channel_id=1, replica_groups=mesh['grp'=4,'dev'=8] {'grp','dev'}, use_global_device_ids=true, to_apply=%region_14.15 | all-reduce | flops 1 | bytes 8 | tf_op jit(solution)/shard_map/psum | solution.py:87
  761.4 0.0 all-to-all-done
  761.4 0.6 copy.77
  (15 shorter events, 0.0 us)
Async XLA Ops:
  7.2 7.1 copy-start.5
  7.2 207.1 %all-gather.7.cloned.1.call-start = ((), (), s32[]{:S(2)}) async-start(), calls=%async_computation.1 | async-start | bytes 34603008 | tf_op jit(solution)/shard_map/all_gather | solution.py:78
  17.2 220.3 %copy-start = (f32[262144]{0:T(1024)S(1)}, f32[262144]{0:T(1024)}, u32[]{:S(2)}) copy-start(f32[262144]{0:T(1024)} %param.17) | copy-start | bytes 3145732
  17.2 220.3 %copy-start.1 = (f32[262144]{0:T(1024)S(1)}, f32[262144]{0:T(1024)}, u32[]{:S(2)}) copy-start(f32[262144]{0:T(1024)} %param.16) | copy-start | bytes 3145732
  17.2 435.7 %all-gather.9.cloned.1.call-start = ((), (), s32[]{:S(2)}) async-start(), calls=%async_computation.2 | async-start | bytes 34603008 | tf_op jit(solution)/shard_map/all_gather | solution.py:78
  241.1 6.3 copy-start.4
  243.4 8.4 %copy-start.7 = (bf16[1024]{0:T(1024)(128)(2,1)S(1)}, bf16[1024]{0:T(1024)(128)(2,1)}, u32[]{:S(2)}) copy-start(bf16[1024]{0:T(1024)(128)(2,1)} %param.13) | copy-start | bytes 6148
  243.4 9.2 %copy-start.6 = (bf16[1024]{0:T(1024)(128)(2,1)S(1)}, bf16[1024]{0:T(1024)(128)(2,1)}, u32[]{:S(2)}) copy-start(bf16[1024]{0:T(1024)(128)(2,1)} %param.14) | copy-start | bytes 6148
  259.2 424.8 %all-gather.11.cloned.1.call-start = ((), (), s32[]{:S(2)}) async-start(), calls=%async_computation.3 | async-start | bytes 34603008 | tf_op jit(solution)/shard_map/all_gather | solution.py:78
  483.1 7.2 copy-start.8
  533.2 174.0 %copy-start.2 = (f32[262144]{0:T(1024)S(1)}, f32[262144]{0:T(1024)}, u32[]{:S(2)}) copy-start(f32[262144]{0:T(1024)} %param.16) | copy-start | bytes 3145732
  709.3 1.0 copy-start.3
  716.8 44.6 %all-to-all-start = ((f32[8,1,128]{2,1,0:T(1,128)}), f32[8,1,128]{2,1,0:T(1,128)S(1)}, u32[]{:S(2)}, u32[]{:S(2)}) async-start(f32[8,1,128]{2,1,0:T(1,128)} %bitcast.22), calls=%async_computation | async-start | bytes 8192 | tf_op jit(solution)/shard_map/all_to_all | solution.py:91
Sparse Core Ops, SparseCore 0:
  17.3 196.8 all-gather.6
  259.3 193.5 all-gather.8
  490.4 193.5 all-gather.10
